TPU v7x, 32 devices: a whole 2x2x4 slice. The times are simulated.
32 devices in a mesh: grp: 4 (over x, core), mem: 8 (over z, y).
Axes of the slice: x: 2, y: 2, z: 4, core: 2. Of those that a mesh axis runs over, the one named last changes fastest.
Arguments:
- source_pts: float32 [64, 8192], P(None, ('grp', 'mem')), may hold values from -30 to 30
- target_pts: float32 [64, 8192], P(None, ('grp', 'mem')), may hold values from -30 to 30
- source_pot: float32 [8192], P(('grp', 'mem')), may hold values from -8 to 520
- target_pot: float32 [8192], P(('grp', 'mem')), may hold values from -8 to 520
- source_logw: float32 [8192], P(('grp', 'mem')), may hold values from -1 to 4
- target_logw: float32 [8192], P(('grp', 'mem')), may hold values from -1 to 4
Outputs:
- source_new: float32 [8192], P(('grp', 'mem'))
- target_new: float32 [8192], P(('grp', 'mem'))
All inputs are finite; a program needn't handle non-finite values.
Results may differ from a plain program's by a relative error of at most 0.0001.
Values sent between devices are 32-bit elements; how exact they have to be, the bound alone decides.
A program may use at most 64 MiB of HBM per device.

v0:
```python
import math
import jax
import jax.numpy as jnp
from jax import lax
from jax.sharding import PartitionSpec as P

epsilon = 4.0
floor_value = -1e30


def sweep(carry, points, squares, row_term, moving, offset):
    count = moving.shape[1]
    limit = 128
    width = math.gcd(count, limit)

    def block(index, state):
        row_max, row_sum, col_max, col_sum = state
        begin = index * width
        cols = lax.dynamic_slice_in_dim(moving, begin, width, 1)
        ycols = cols[:-1]
        cvals = cols[-1]
        ysq = 0.5 * jnp.sum(ycols * ycols, 0)
        cross = lax.dot_general(
            points,
            ycols,
            (((0,), (0,)), ((), ())),
            precision=lax.Precision.HIGHEST,
            preferred_element_type=jnp.float32,
        )
        half = (squares[:, None] + ysq[None, :] - cross) / epsilon
        scores = cvals[None, :] - half
        new_row = jnp.maximum(row_max, jnp.max(scores, 1))
        row_sum = row_sum * jnp.exp(row_max - new_row) + jnp.sum(
            jnp.exp(scores - new_row[:, None]), 1
        )
        others = row_term[:, None] - half
        place = offset + begin
        old_max = lax.dynamic_slice_in_dim(col_max, place, width, 0)
        old_sum = lax.dynamic_slice_in_dim(col_sum, place, width, 0)
        new_col = jnp.maximum(old_max, jnp.max(others, 0))
        new_sum = old_sum * jnp.exp(old_max - new_col) + jnp.sum(
            jnp.exp(others - new_col[None, :]), 0
        )
        col_max = lax.dynamic_update_slice_in_dim(col_max, new_col, place, 0)
        col_sum = lax.dynamic_update_slice_in_dim(col_sum, new_sum, place, 0)
        return (new_row, row_sum, col_max, col_sum)

    return lax.fori_loop(0, count // width, block, carry)


def totals(source_logw, target_logw):
    peaks = lax.pmax((jnp.max(source_logw), jnp.max(target_logw)), ("grp", "mem"))
    masses = lax.psum(
        (jnp.sum(jnp.exp(source_logw - peaks[0])), jnp.sum(jnp.exp(target_logw - peaks[1]))),
        ("grp", "mem"),
    )
    return (peaks[0] + jnp.log(masses[0]), peaks[1] + jnp.log(masses[1]))


def local(source_pts, target_pts, source_pot, target_pot, source_logw, target_logw):
    members = lax.axis_size("mem")
    rows = source_pts.shape[1]
    outer = rows * members
    src_norm, tgt_norm = totals(source_logw, target_logw)
    row_term = source_logw - src_norm + source_pot / epsilon
    col_term = target_logw - tgt_norm + target_pot / epsilon
    moving = jnp.concatenate([target_pts, col_term[None, :]], 0)
    standing = jnp.concatenate([source_pts, row_term[None, :]], 0)
    row_block = lax.all_gather(standing, "mem", axis=1, tiled=True)
    col_block = lax.all_gather(moving, "grp", axis=1, tiled=True)
    block_pts = row_block[:-1]
    block_terms = row_block[-1]
    block_sq = 0.5 * jnp.sum(block_pts * block_pts, 0)
    span = col_block.shape[1]
    carry = (
        jnp.full((outer,), floor_value, jnp.float32),
        jnp.zeros((outer,), jnp.float32),
        jnp.full((span,), floor_value, jnp.float32),
        jnp.zeros((span,), jnp.float32),
    )
    row_max, row_sum, col_max, col_sum = sweep(
        carry, block_pts, block_sq, block_terms, col_block, 0
    )
    rpeak = lax.pmax(row_max, "mem")
    own_rsum = lax.psum_scatter(
        row_sum * jnp.exp(row_max - rpeak), "mem", scatter_dimension=0, tiled=True
    )
    own_rmax = lax.dynamic_slice_in_dim(rpeak, lax.axis_index("mem") * rows, rows, 0)
    row_total = own_rmax + jnp.log(own_rsum)
    cpeak = lax.pmax(col_max, "grp")
    own_sum = lax.psum_scatter(
        col_sum * jnp.exp(col_max - cpeak), "grp", scatter_dimension=0, tiled=True
    )
    own_max = lax.dynamic_slice_in_dim(cpeak, lax.axis_index("grp") * rows, rows, 0)
    col_total = own_max + jnp.log(own_sum)
    row_hat = -epsilon * row_total
    col_hat = -epsilon * col_total
    return (0.5 * (source_pot + row_hat), 0.5 * (target_pot + col_hat))


def solution(mesh):
    return jax.shard_map(
        local,
        mesh=mesh,
        in_specs=(
            P(None, ("grp", "mem")),
            P(None, ("grp", "mem")),
            P(("grp", "mem")),
            P(("grp", "mem")),
            P(("grp", "mem")),
            P(("grp", "mem")),
        ),
        out_specs=(P(("grp", "mem")), P(("grp", "mem"))),
        check_vma=False,
    )
```

profile of v0, /device:TPU:0, one launch (start us, length us, event | category | flops | bytes accessed | tf_op | source)
XLA Modules:
  0.0 205.6 jit_solution(15678545301726195394)
XLA Ops:
  0.6 1.3 reduce_max.44
  1.9 0.6 reduce_max.45
  2.5 42.2 %all-reduce.3 = (f32[]{:T(128)}, f32[]{:T(128)}) all-reduce(f32[]{:T(128)} %reduce_max.44, f32[]{:T(128)} %reduce_max.45), channel_id=1, replica_groups=mesh['grp'=4,'mem'=8] {'grp','mem'}, use_global_device_ids=true, to_apply=%region_1.0 | all-reduce | flops 2 | bytes 16 | tf_op jit(solution)/shard_map/pmax | solution.py:52
  44.8 0.7 copy-done.3
  45.4 2.0 exponential_reduce_fusion.2
  47.4 40.6 %all-reduce.2 = (f32[]{:T(128)}, f32[]{:T(128)}) all-reduce(f32[]{:T(128)} %get-tuple-element.225, f32[]{:T(128)} %get-tuple-element.224), channel_id=1, replica_groups=mesh['grp'=4,'mem'=8] {'grp','mem'}, use_global_device_ids=true, to_apply=%region_3.0 | all-reduce | flops 2 | bytes 16 | tf_op jit(solution)/shard_map/psum | solution.py:53
  89.3 0.8 pad_maximum_fusion.1
  90.2 31.4 %all_gather.7 = f32[65,2048]{1,0:T(8,128)S(1)} all-gather(f32[65,256]{1,0:T(8,128)S(1)} %pad_maximum_fusion.1), channel_id=1, replica_groups=mesh['grp'=4,'mem'=8] {'mem'}, dimensions={1}, use_global_device_ids=true | all-gather | bytes 599040 | tf_op jit(solution)/shard_map/all_gather | solution.py:69
  121.7 0.7 copy-done
  123.8 6.7 %all_gather.6 = f32[65,1024]{1,0:T(8,128)S(1)} all-gather(f32[65,256]{1,0:T(8,128)S(1)} %pad_maximum_fusion), channel_id=1, replica_groups=mesh['grp'=4,'mem'=8] {'grp'}, dimensions={1}, use_global_device_ids=true | all-gather | bytes 332800 | tf_op jit(solution)/shard_map/all_gather | solution.py:70
  130.5 0.7 slice-done
  131.2 18.0 %while.20 = (s32[]{:T(128)}, f32[2048]{0:T(1024)S(1)}, f32[2048]{0:T(1024)S(1)}, f32[1024]{0:T(1024)S(1)}, f32[1024]{0:T(1024)S(1)}, /*index=5*/f32[65,1024]{1,0...) while((s32[]{:T(128)}, f32[2048]{0:T(1024)S(1)}, ...), condition=%wide.region_15.0_spmd.clone, body=%wide.region_9.0_spmd.clone.sunk | while | flops 204761344 | bytes 2844898 | solution.py:48
  131.2 1.3 subtract_reduce_fusion.3
  132.6 0.2 fusion.20
  132.7 0.4 exponential_reduce_fusion.5
  133.2 0.2 add_dynamic-update-slice_fusion.2
  133.5 1.3 subtract_reduce_fusion.3
  134.8 0.2 fusion.20
  135.0 0.4 exponential_reduce_fusion.5
  135.4 0.2 add_dynamic-update-slice_fusion.2
  135.7 1.3 subtract_reduce_fusion.3
  137.1 0.2 fusion.20
  137.3 0.4 exponential_reduce_fusion.5
  138.0 1.3 subtract_reduce_fusion.3
  139.3 0.2 fusion.20
  139.5 0.4 exponential_reduce_fusion.5
  140.2 1.3 subtract_reduce_fusion.3
  141.6 0.2 fusion.20
  141.8 0.4 exponential_reduce_fusion.5
  142.5 1.3 subtract_reduce_fusion.3
  143.8 0.2 fusion.20
  144.0 0.4 exponential_reduce_fusion.5
  144.8 1.3 subtract_reduce_fusion.3
  146.1 0.2 fusion.20
  146.3 0.4 exponential_reduce_fusion.5
  147.0 1.3 subtract_reduce_fusion.3
  148.3 0.2 fusion.20
  148.5 0.4 exponential_reduce_fusion.5
  149.2 7.1 %pmax.31 = f32[1024]{0:T(1024)S(1)} all-reduce(f32[1024]{0:T(1024)S(1)} %get-tuple-element.161), channel_id=1, replica_groups=mesh['grp'=4,'mem'=8] {'grp'}, use_global_device_ids=true, to_apply=%region_18.0 | all-reduce | flops 1024 | bytes 8192 | tf_op jit(solution)/shard_map/pmax | solution.py:90
  156.3 6.0 %all-reduce.1 = f32[1024]{0:T(1024)S(1)} all-reduce(f32[1024]{0:T(1024)S(1)} %exponential_multiply_fusion.1), channel_id=3, replica_groups=mesh['grp'=4,'mem'=8] {'grp'}, use_global_device_ids=true, to_apply=%region_19.0.clone | all-reduce | flops 1024 | bytes 8192
  162.3 0.6 copy-done.7
  162.9 0.6 dynamic-slice.2
  164.2 0.7 fusion.12
  164.8 20.8 %pmax.30 = f32[2048]{0:T(1024)S(1)} all-reduce(f32[2048]{0:T(1024)S(1)} %get-tuple-element.159), channel_id=1, replica_groups=mesh['grp'=4,'mem'=8] {'mem'}, use_global_device_ids=true, to_apply=%region_16.0 | all-reduce | flops 2048 | bytes 16384 | tf_op jit(solution)/shard_map/pmax | solution.py:84
  185.7 17.4 %all-reduce = f32[2048]{0:T(1024)S(1)} all-reduce(f32[2048]{0:T(1024)S(1)} %exponential_multiply_fusion), channel_id=2, replica_groups=mesh['grp'=4,'mem'=8] {'mem'}, use_global_device_ids=true, to_apply=%region_17.0.clone | all-reduce | flops 2048 | bytes 16384
  203.1 0.6 copy-done.6
  203.7 0.6 dynamic-slice
  205.0 0.7 fusion.11
  (94 shorter events, 1.9 us)
Async XLA Ops:
  0.6 1.3 copy-start.2
  44.8 0.7 copy-start.3
  88.6 0.7 copy-start.5
  121.6 0.8 copy-start
  121.6 2.1 %copy-start.1 = (f32[64,256]{1,0:T(8,128)S(1)}, f32[64,256]{1,0:T(8,128)}, u32[]{:S(2)}) copy-start(f32[64,256]{1,0:T(8,128)} %param.9) | copy-start | bytes 196612
  123.0 0.7 copy-start.4
  130.5 0.7 slice-start
  162.3 0.7 copy-start.7
  203.1 0.7 copy-start.6
where the time goes:
time: 206 us
  blocking collectives  172 us (83%)
  other arithmetic  13 us (6%)
  matrix products  10.4 us (5%)
  local copies, waits for them, and re-layouts  4.74 us (2%)
  between operations  4.67 us (2%)
    pmax x1, blocking collectives, totals(): lax.pmax((jnp.max(source_logw), jnp.max(target_logw)), ('grp', 'mem'))  42.2 us
    psum x1, blocking collectives, totals(): lax.psum((jnp.sum(jnp.exp(source_logw - peaks[0])), jnp.sum(jnp.exp(targe...  40.6 us
    all_gather x1, blocking collectives, local(): row_block = lax.all_gather(standing, 'mem', axis=1, tiled=True)  31.4 us
    unnamed x2, blocking collectives  23.4 us
    pmax x1, blocking collectives, local(): rpeak = lax.pmax(row_max, 'mem')  20.8 us
    dot_general x8, matrix products, block(): lax.dot_general(points, ycols, (((0,), (0,)), ((), ())), precision=lax.Pr...  10.4 us
    pmax x1, blocking collectives, local(): cpeak = lax.pmax(col_max, 'grp')  7.05 us
    all_gather x1, blocking collectives, local(): col_block = lax.all_gather(moving, 'grp', axis=1, tiled=True)  6.72 us

commit v1 on v0

--- a/solution.py
+++ b/solution.py
@@ -50,10 +50,10 @@
 
 def totals(source_logw, target_logw):
     peaks = lax.pmax((jnp.max(source_logw), jnp.max(target_logw)), ("grp", "mem"))
-    masses = lax.psum(
-        (jnp.sum(jnp.exp(source_logw - peaks[0])), jnp.sum(jnp.exp(target_logw - peaks[1]))),
-        ("grp", "mem"),
+    inner = lax.psum(
+        (jnp.sum(jnp.exp(source_logw - peaks[0])), jnp.sum(jnp.exp(target_logw - peaks[1]))), "grp"
     )
+    masses = lax.psum(inner, "mem")
     return (peaks[0] + jnp.log(masses[0]), peaks[1] + jnp.log(masses[1]))
 
 

time: 206 us -> 191 us (0.927)
  blocking collectives: 172 us -> 157 us
    psum x1, blocking collectives: 40.6 us -> 6.51 us  [totals(): lax.psum((jnp.sum(jnp.exp(source_logw - peaks[0])), jnp.sum(jnp.exp(targe...]
    psum x0 -> x1, blocking collectives: none -> 22 us  [totals(): masses = lax.psum(inner, 'mem')]
    pmax x1, blocking collectives: 20.8 us -> 17.4 us  [local(): rpeak = lax.pmax(row_max, 'mem')]
where the time goes in v1:
time: 191 us; the launch traced here: 190 us
  blocking collectives  157 us (82%)
  other arithmetic  13 us (7%)
  matrix products  10.4 us (5%)
  local copies, waits for them, and re-layouts  4.74 us (2%)
  between operations  4.67 us (2%)
    pmax x1, blocking collectives, totals(): lax.pmax((jnp.max(source_logw), jnp.max(target_logw)), ('grp', 'mem'))  42.2 us
    all_gather x1, blocking collectives, local(): row_block = lax.all_gather(standing, 'mem', axis=1, tiled=True)  31.6 us
    unnamed x2, blocking collectives  25.1 us
    psum x1, blocking collectives, totals(): masses = lax.psum(inner, 'mem')  22 us
    pmax x1, blocking collectives, local(): rpeak = lax.pmax(row_max, 'mem')  17.4 us
    dot_general x8, matrix products, block(): lax.dot_general(points, ycols, (((0,), (0,)), ((), ())), precision=lax.Pr...  10.4 us
    psum x1, blocking collectives, totals(): lax.psum((jnp.sum(jnp.exp(source_logw - peaks[0])), jnp.sum(jnp.exp(targe...  6.51 us
    pmax x1, blocking collectives, local(): cpeak = lax.pmax(col_max, 'grp')  6.2 us

profile of v1, /device:TPU:0, one launch (start us, length us, event | category | flops | bytes accessed | tf_op | source)
XLA Modules:
  0.0 190.2 jit_solution(13796606693855869674)
XLA Ops:
  0.6 1.3 reduce_max.44
  1.9 0.6 reduce_max.45
  2.5 42.2 %all-reduce.2 = (f32[]{:T(128)}, f32[]{:T(128)}) all-reduce(f32[]{:T(128)} %reduce_max.44, f32[]{:T(128)} %reduce_max.45), channel_id=1, replica_groups=mesh['grp'=4,'mem'=8] {'grp','mem'}, use_global_device_ids=true, to_apply=%region_1.0 | all-reduce | flops 2 | bytes 16 | tf_op jit(solution)/shard_map/pmax | solution.py:52
  44.7 0.7 copy-done.3
  45.4 2.0 %exponential_reduce_fusion.2 = (f32[]{:T(128)}, f32[]{:T(128)}) fusion(f32[256]{0:T(256)S(1)} %copy-done.2, f32[]{:T(128)} %get-tuple-element.216, f32[256]{0:T(256)S(1)} %copy-done.3, f32[]{:T(128)} %get-tuple-element.215), kind=kLoop, calls=%fused_computation.32 | loop fusion | flops 1022 | bytes 2064 | tf_op jit(solution)/shard_map/reduce_sum | solution.py:54
  47.4 6.5 %all-reduce.4 = (f32[]{:T(128)}, f32[]{:T(128)}) all-reduce(f32[]{:T(128)} %get-tuple-element.227, f32[]{:T(128)} %get-tuple-element.226), channel_id=1, replica_groups=mesh['grp'=4,'mem'=8] {'grp'}, use_global_device_ids=true, to_apply=%region_3.0 | all-reduce | flops 2 | bytes 16 | tf_op jit(solution)/shard_map/psum | solution.py:53
  53.9 22.0 %all-reduce.3 = (f32[]{:T(128)}, f32[]{:T(128)}) all-reduce(f32[]{:T(128)} %get-tuple-element.219, f32[]{:T(128)} %get-tuple-element.220), channel_id=1, replica_groups=mesh['grp'=4,'mem'=8] {'mem'}, use_global_device_ids=true, to_apply=%region_4.0 | all-reduce | flops 2 | bytes 16 | tf_op jit(solution)/shard_map/psum | solution.py:56
  77.2 0.8 pad_maximum_fusion.1
  78.1 31.6 %all_gather.7 = f32[65,2048]{1,0:T(8,128)S(1)} all-gather(f32[65,256]{1,0:T(8,128)S(1)} %pad_maximum_fusion.1), channel_id=1, replica_groups=mesh['grp'=4,'mem'=8] {'mem'}, dimensions={1}, use_global_device_ids=true | all-gather | bytes 599040 | tf_op jit(solution)/shard_map/all_gather | solution.py:69
  109.7 0.7 copy-done
  111.8 5.9 %all_gather.6 = f32[65,1024]{1,0:T(8,128)S(1)} all-gather(f32[65,256]{1,0:T(8,128)S(1)} %pad_maximum_fusion), channel_id=1, replica_groups=mesh['grp'=4,'mem'=8] {'grp'}, dimensions={1}, use_global_device_ids=true | all-gather | bytes 332800 | tf_op jit(solution)/shard_map/all_gather | solution.py:70
  117.7 0.7 slice-done
  118.3 18.0 %while.20 = (s32[]{:T(128)}, f32[2048]{0:T(1024)S(1)}, f32[2048]{0:T(1024)S(1)}, f32[1024]{0:T(1024)S(1)}, f32[1024]{0:T(1024)S(1)}, /*index=5*/f32[65,1024]{1,0...) while((s32[]{:T(128)}, f32[2048]{0:T(1024)S(1)}, ...), condition=%wide.region_17.0_spmd.clone, body=%wide.region_11.0_spmd.clone.sunk | while | flops 204761344 | bytes 2844898 | solution.py:48
  118.4 1.3 subtract_reduce_fusion.3
  119.7 0.2 fusion.20
  119.9 0.4 exponential_reduce_fusion.5
  120.3 0.2 add_dynamic-update-slice_fusion.2
  120.6 1.3 subtract_reduce_fusion.3
  122.0 0.2 fusion.20
  122.2 0.4 exponential_reduce_fusion.5
  122.9 1.3 subtract_reduce_fusion.3
  124.2 0.2 fusion.20
  124.4 0.4 exponential_reduce_fusion.5
  125.2 1.3 subtract_reduce_fusion.3
  126.5 0.2 fusion.20
  126.7 0.4 exponential_reduce_fusion.5
  127.4 1.3 subtract_reduce_fusion.3
  128.7 0.2 fusion.20
  128.9 0.4 exponential_reduce_fusion.5
  129.7 1.3 subtract_reduce_fusion.3
  131.0 0.2 fusion.20
  131.2 0.4 exponential_reduce_fusion.5
  131.9 1.3 subtract_reduce_fusion.3
  133.3 0.2 fusion.20
  133.4 0.4 exponential_reduce_fusion.5
  134.2 1.3 subtract_reduce_fusion.3
  135.5 0.2 fusion.20
  135.7 0.4 exponential_reduce_fusion.5
  136.4 6.2 %pmax.31 = f32[1024]{0:T(1024)S(1)} all-reduce(f32[1024]{0:T(1024)S(1)} %get-tuple-element.161), channel_id=1, replica_groups=mesh['grp'=4,'mem'=8] {'grp'}, use_global_device_ids=true, to_apply=%region_20.0 | all-reduce | flops 1024 | bytes 8192 | tf_op jit(solution)/shard_map/pmax | solution.py:90
  142.6 5.7 %all-reduce.1 = f32[1024]{0:T(1024)S(1)} all-reduce(f32[1024]{0:T(1024)S(1)} %exponential_multiply_fusion.1), channel_id=3, replica_groups=mesh['grp'=4,'mem'=8] {'grp'}, use_global_device_ids=true, to_apply=%region_21.0.clone | all-reduce | flops 1024 | bytes 8192
  148.3 0.6 copy-done.7
  148.9 0.6 dynamic-slice.2
  150.1 0.7 fusion.12
  150.8 17.4 %pmax.30 = f32[2048]{0:T(1024)S(1)} all-reduce(f32[2048]{0:T(1024)S(1)} %get-tuple-element.159), channel_id=1, replica_groups=mesh['grp'=4,'mem'=8] {'mem'}, use_global_device_ids=true, to_apply=%region_18.0 | all-reduce | flops 2048 | bytes 16384 | tf_op jit(solution)/shard_map/pmax | solution.py:84
  168.2 19.4 %all-reduce = f32[2048]{0:T(1024)S(1)} all-reduce(f32[2048]{0:T(1024)S(1)} %exponential_multiply_fusion), channel_id=2, replica_groups=mesh['grp'=4,'mem'=8] {'mem'}, use_global_device_ids=true, to_apply=%region_19.0.clone | all-reduce | flops 2048 | bytes 16384
  187.6 0.6 copy-done.6
  188.3 0.6 dynamic-slice
  189.5 0.7 fusion.11
  (95 shorter events, 2.0 us)
Async XLA Ops:
  0.6 1.3 copy-start.2
  44.7 0.7 copy-start.3
  76.6 0.7 copy-start.5
  109.6 0.8 copy-start
  109.7 2.1 %copy-start.1 = (f32[64,256]{1,0:T(8,128)S(1)}, f32[64,256]{1,0:T(8,128)}, u32[]{:S(2)}) copy-start(f32[64,256]{1,0:T(8,128)} %param.9) | copy-start | bytes 196612
  111.1 0.7 copy-start.4
  117.7 0.7 slice-start
  148.2 0.7 copy-start.7
  187.6 0.7 copy-start.6
